TPU v7x, 32 devices: a whole 2x2x4 slice. The times are simulated.
32 devices in a mesh: dp: 8 (over y, x, core), tensor: 4 (over z).
Axes of the slice: x: 2, y: 2, z: 4, core: 2. Of those that a mesh axis runs over, the one named last changes fastest.
Arguments:
- tokens: bfloat16 [4096, 1024], P(('dp', 'tensor')), may hold values from -5 to 5
- lengths: int32 [8, 2], P('dp'), may hold values from 0 to 512, as said below
- w_query: bfloat16 [1024, 1024], P('dp', 'tensor'), may hold values from -0.1875 to 0.1875
- b_query: float32 [1024], replicated, may hold values from -3 to 3
- w_key: bfloat16 [1024, 1024], P('dp', 'tensor'), may hold values from -0.1875 to 0.1875
- w_value: bfloat16 [1024, 1024], P('dp', 'tensor'), may hold values from -0.1875 to 0.1875
- b_value: float32 [1024], replicated, may hold values from -3 to 3
- w_out: bfloat16 [1024, 1024], P('tensor', 'dp'), may hold values from -3 to 3
- b_out: float32 [1024], replicated, may hold values from -3 to 3
- gain_attn: float32 [1024], replicated, may hold values from 0.1 to 1.9
- shift_attn: float32 [1024], replicated, may hold values from -3 to 3
- w_in: bfloat16 [1024, 4096], P('dp', 'tensor'), may hold values from -0.1875 to 0.1875
- b_in: float32 [4096], replicated, may hold values from -3 to 3
- w_back: bfloat16 [4096, 1024], P('tensor', 'dp'), may hold values from -0.09375 to 0.09375
- b_back: float32 [1024], replicated, may hold values from -3 to 3
- gain_ffn: float32 [1024], replicated, may hold values from 0.1 to 1.9
- shift_ffn: float32 [1024], replicated, may hold values from -3 to 3
- cotangent: bfloat16 [4096, 1024], P(('dp', 'tensor')), may hold values from -6 to 6
Outputs:
- output: bfloat16 [4096, 1024], P(('dp', 'tensor'))
- grad_tokens: float32 [4096, 1024], P(('dp', 'tensor'))
- grad_w_query: float32 [1024, 1024], P('dp', 'tensor')
- grad_b_query: float32 [1024], replicated
- grad_w_key: float32 [1024, 1024], P('dp', 'tensor')
- grad_w_value: float32 [1024, 1024], P('dp', 'tensor')
- grad_b_value: float32 [1024], replicated
- grad_w_out: float32 [1024, 1024], P('tensor', 'dp')
- grad_b_out: float32 [1024], replicated
- grad_gain_attn: float32 [1024], replicated
- grad_shift_attn: float32 [1024], replicated
- grad_w_in: float32 [1024, 4096], P('dp', 'tensor')
- grad_b_in: float32 [4096], replicated
- grad_w_back: float32 [4096, 1024], P('tensor', 'dp')
- grad_b_back: float32 [1024], replicated
- grad_gain_ffn: float32 [1024], replicated
- grad_shift_ffn: float32 [1024], replicated
Inputs may be any that keep to these rules, and one draw needn't show every extreme that they name: Each group's 2 lengths sum to at most 512; the first is 1 or more, the second may be 0; in every draw one group holds a single sequence of exactly 512 tokens.
All inputs are finite; a program needn't handle non-finite values.
Results may differ from a plain program's by a relative error of at most 0.02.
Values may be sent and summed in bfloat16 or wider, within the bound.
A program may use at most 128 MiB of HBM per device.

v0:
```python
import jax
import jax.numpy as jnp
from jax import lax
from jax.sharding import PartitionSpec as P

HD = 64
epsilon = 1e-06
masked_value = -1e30


def matmul_plain(left_side, right_side):
    return jnp.dot(left_side, right_side, preferred_element_type=jnp.float32)


def matmul_over_rows(left_side, right_side):
    return lax.dot_general(
        left_side, right_side, (((0,), (0,)), ((), ())), preferred_element_type=jnp.float32
    )


def matmul_over_cols(left_side, right_side):
    return lax.dot_general(
        left_side, right_side, (((1,), (1,)), ((), ())), preferred_element_type=jnp.float32
    )


def layer_norm(residual, gain_vec, shift_vec):
    mean_val = jnp.mean(residual, axis=-1, keepdims=True)
    centered = residual - mean_val
    inv_std = lax.rsqrt(jnp.mean(centered * centered, axis=-1, keepdims=True) + epsilon)
    normed = centered * inv_std
    return (normed * gain_vec + shift_vec, normed, inv_std)


def norm_back(grad_out, normed, inv_std, gain_vec):
    grad_norm = grad_out * gain_vec
    first_mean = jnp.mean(grad_norm, axis=-1, keepdims=True)
    second_mean = jnp.mean(grad_norm * normed, axis=-1, keepdims=True)
    return inv_std * (grad_norm - first_mean - normed * second_mean)


def gelu_parts(preact):
    cdf_val = 0.5 * (1.0 + lax.erf(preact * 0.7071067811865476))
    pdf_val = jnp.exp(-0.5 * preact * preact) * 0.3989422804014327
    return (preact * cdf_val, cdf_val + preact * pdf_val)


def attend_forward(query_rows, key_rows, value_rows, seg_ids, head_dim, block_rows):
    group_rows, head_cols = query_rows.shape
    pair_width = 2 * head_dim
    block_count = group_rows // block_rows
    pair_count = head_cols // pair_width
    score_scale = head_dim ** (-0.5)

    def attend_step(step_index, loop_carry):
        context, log_total = loop_carry
        pair_index = step_index // block_count
        row_start = step_index % block_count * block_rows
        first_col = pair_index * pair_width
        query_block = lax.dynamic_slice(
            query_rows, (row_start, first_col), (block_rows, pair_width)
        ).reshape(block_rows, 2, head_dim)
        key_pair = lax.dynamic_slice(key_rows, (0, first_col), (group_rows, pair_width)).reshape(
            group_rows, 2, head_dim
        )
        value_pair = lax.dynamic_slice(
            value_rows, (0, first_col), (group_rows, pair_width)
        ).reshape(group_rows, 2, head_dim)
        same_seg = seg_ids[:, None] == seg_ids[None, :]
        scores = (
            jnp.einsum("qhd,khd->hqk", query_block, key_pair, preferred_element_type=jnp.float32)
            * score_scale
        )
        scores = jnp.where(same_seg[None], scores, masked_value)
        row_max = jnp.max(scores, axis=-1, keepdims=True)
        block_total = row_max + jnp.log(jnp.sum(jnp.exp(scores - row_max), axis=-1, keepdims=True))
        prob_bf = jnp.exp(scores - block_total).astype(jnp.bfloat16)
        context_block = jnp.einsum(
            "hqk,khd->qhd", prob_bf, value_pair, preferred_element_type=jnp.float32
        ).astype(jnp.bfloat16)
        context = lax.dynamic_update_slice(
            context, context_block.reshape(block_rows, pair_width), (row_start, first_col)
        )
        log_total = lax.dynamic_update_slice(
            log_total, block_total[:, :, 0], (2 * pair_index, row_start)
        )
        return (context, log_total)

    start_carry = (
        jnp.zeros((group_rows, head_cols), jnp.bfloat16),
        jnp.zeros((head_cols // head_dim, group_rows), jnp.float32),
    )
    return lax.fori_loop(0, pair_count * block_count, attend_step, start_carry)


def attend_backward(
    query_rows,
    key_rows,
    value_rows,
    context,
    grad_context,
    log_total,
    seg_ids,
    head_dim,
    block_rows,
):
    group_rows, head_cols = query_rows.shape
    pair_width = 2 * head_dim
    block_count = group_rows // block_rows
    pair_count = head_cols // pair_width
    score_scale = head_dim ** (-0.5)

    def back_step(step_index, loop_carry):
        grad_query, grad_keys, grad_values = loop_carry
        pair_index = step_index // block_count
        row_start = step_index % block_count * block_rows
        first_col = pair_index * pair_width
        query_block = lax.dynamic_slice(
            query_rows, (row_start, first_col), (block_rows, pair_width)
        ).reshape(block_rows, 2, head_dim)
        key_pair = lax.dynamic_slice(key_rows, (0, first_col), (group_rows, pair_width)).reshape(
            group_rows, 2, head_dim
        )
        value_pair = lax.dynamic_slice(
            value_rows, (0, first_col), (group_rows, pair_width)
        ).reshape(group_rows, 2, head_dim)
        context_block = lax.dynamic_slice(
            context, (row_start, first_col), (block_rows, pair_width)
        ).reshape(block_rows, 2, head_dim)
        gctx_block = lax.dynamic_slice(
            grad_context, (row_start, first_col), (block_rows, pair_width)
        ).reshape(block_rows, 2, head_dim)
        total_block = lax.dynamic_slice(log_total, (2 * pair_index, row_start), (2, block_rows))
        same_seg = seg_ids[:, None] == seg_ids[None, :]
        scores = (
            jnp.einsum("qhd,khd->hqk", query_block, key_pair, preferred_element_type=jnp.float32)
            * score_scale
        )
        scores = jnp.where(same_seg[None], scores, masked_value)
        probs = jnp.exp(scores - total_block[:, :, None])
        prob_bf = probs.astype(jnp.bfloat16)
        grad_probs = jnp.einsum(
            "qhd,khd->hqk", gctx_block, value_pair, preferred_element_type=jnp.float32
        )
        delta_rows = jnp.sum(
            gctx_block.astype(jnp.float32) * context_block.astype(jnp.float32), axis=-1
        ).T[:, :, None]
        grad_scores = (probs * (grad_probs - delta_rows) * score_scale).astype(jnp.bfloat16)
        grad_q_block = jnp.einsum(
            "hqk,khd->qhd", grad_scores, key_pair, preferred_element_type=jnp.float32
        ).reshape(block_rows, pair_width)
        grad_k_pair = jnp.einsum(
            "hqk,qhd->khd", grad_scores, query_block, preferred_element_type=jnp.float32
        ).reshape(group_rows, pair_width)
        grad_v_pair = jnp.einsum(
            "hqk,qhd->khd", prob_bf, gctx_block, preferred_element_type=jnp.float32
        ).reshape(group_rows, pair_width)
        grad_query = lax.dynamic_update_slice(grad_query, grad_q_block, (row_start, first_col))
        old_keys = lax.dynamic_slice(grad_keys, (0, first_col), (group_rows, pair_width))
        grad_keys = lax.dynamic_update_slice(grad_keys, old_keys + grad_k_pair, (0, first_col))
        old_values = lax.dynamic_slice(grad_values, (0, first_col), (group_rows, pair_width))
        grad_values = lax.dynamic_update_slice(
            grad_values, old_values + grad_v_pair, (0, first_col)
        )
        return (grad_query, grad_keys, grad_values)

    zero_grad = jnp.zeros((group_rows, head_cols), jnp.float32)
    return lax.fori_loop(0, pair_count * block_count, back_step, (zero_grad, zero_grad, zero_grad))


def on_device(
    tokens,
    lengths,
    w_query,
    b_query,
    w_key,
    w_value,
    b_value,
    w_out,
    b_out,
    gain_attn,
    shift_attn,
    w_in,
    b_in,
    w_back,
    b_back,
    gain_ffn,
    shift_ffn,
    cotangent,
):
    tensor_size = lax.axis_size("tensor")
    tensor_index = lax.axis_index("tensor")
    local_rows = tokens.shape[0]
    group_rows = local_rows * tensor_size
    head_cols = w_query.shape[1]
    hidden_cols = w_in.shape[1]
    block_rows = min(512, group_rows)
    seq_lens = lengths[0]
    live_end = seq_lens[0] + seq_lens[1]
    positions = jnp.arange(group_rows, dtype=jnp.int32)
    seg_ids = (positions >= seq_lens[0]).astype(jnp.int32) + (positions >= live_end).astype(
        jnp.int32
    )
    local_pos = tensor_index * local_rows + jnp.arange(local_rows, dtype=jnp.int32)
    live_rows = (local_pos < live_end).astype(jnp.float32)[:, None]
    rows_full = lax.all_gather(tokens, "tensor", axis=0, tiled=True)
    attn_mats = (
        lax.all_gather(w_query, "dp", axis=0, tiled=True),
        lax.all_gather(w_key, "dp", axis=0, tiled=True),
        lax.all_gather(w_value, "dp", axis=0, tiled=True),
        lax.all_gather(w_out, "dp", axis=1, tiled=True),
    )
    mat_query, mat_key, mat_value, mat_out = attn_mats
    bias_query = lax.dynamic_slice_in_dim(b_query, tensor_index * head_cols, head_cols)
    bias_value = lax.dynamic_slice_in_dim(b_value, tensor_index * head_cols, head_cols)
    bias_in = lax.dynamic_slice_in_dim(b_in, tensor_index * hidden_cols, hidden_cols)
    query_rows = (matmul_plain(rows_full, mat_query) + bias_query).astype(jnp.bfloat16)
    key_rows = matmul_plain(rows_full, mat_key).astype(jnp.bfloat16)
    value_rows = (matmul_plain(rows_full, mat_value) + bias_value).astype(jnp.bfloat16)
    context, log_total = attend_forward(query_rows, key_rows, value_rows, seg_ids, HD, block_rows)
    attn_sum = lax.psum_scatter(
        matmul_plain(context, mat_out).astype(jnp.bfloat16),
        "tensor",
        scatter_dimension=0,
        tiled=True,
    ).astype(jnp.float32)
    resid_one = tokens.astype(jnp.float32) + attn_sum + b_out
    hidden_one, normed_one, inv_one = layer_norm(resid_one, gain_attn, shift_attn)
    hidden_bf = hidden_one.astype(jnp.bfloat16)
    hidden_full = lax.all_gather(hidden_bf, "tensor", axis=0, tiled=True)
    ffn_mats = (
        lax.all_gather(w_in, "dp", axis=0, tiled=True),
        lax.all_gather(w_back, "dp", axis=1, tiled=True),
    )
    mat_in, mat_back = ffn_mats
    preact = matmul_plain(hidden_full, mat_in) + bias_in
    activ_val, gelu_slope = gelu_parts(preact)
    activation = activ_val.astype(jnp.bfloat16)
    ffn_sum = lax.psum_scatter(
        matmul_plain(activation, mat_back).astype(jnp.bfloat16),
        "tensor",
        scatter_dimension=0,
        tiled=True,
    ).astype(jnp.float32)
    resid_two = hidden_one + ffn_sum + b_back
    normed_out, normed_two, inv_two = layer_norm(resid_two, gain_ffn, shift_ffn)
    output = (normed_out * live_rows).astype(jnp.bfloat16)
    grad_final = cotangent.astype(jnp.float32) * live_rows
    grad_gain_ffn = jnp.sum(grad_final * normed_two, axis=0)
    grad_shift_ffn = jnp.sum(grad_final, axis=0)
    grad_two = norm_back(grad_final, normed_two, inv_two, gain_ffn)
    grad_b_back = jnp.sum(grad_two, axis=0)
    mat_query, mat_key, mat_value, mat_out, mat_in, mat_back = (
        lax.all_gather(w_query, "dp", axis=0, tiled=True),
        lax.all_gather(w_key, "dp", axis=0, tiled=True),
        lax.all_gather(w_value, "dp", axis=0, tiled=True),
        lax.all_gather(w_out, "dp", axis=1, tiled=True),
        lax.all_gather(w_in, "dp", axis=0, tiled=True),
        lax.all_gather(w_back, "dp", axis=1, tiled=True),
    )
    grad_two_full = lax.all_gather(grad_two.astype(jnp.bfloat16), "tensor", axis=0, tiled=True)
    grad_w_back = matmul_over_rows(activation, grad_two_full)
    grad_pre = matmul_over_cols(grad_two_full, mat_back) * gelu_slope
    grad_b_in_part = jnp.sum(grad_pre, axis=0)
    grad_pre_bf = grad_pre.astype(jnp.bfloat16)
    grad_w_in = matmul_over_rows(hidden_full, grad_pre_bf)
    grad_one_out = grad_two + lax.psum_scatter(
        matmul_over_cols(grad_pre_bf, mat_in).astype(jnp.bfloat16),
        "tensor",
        scatter_dimension=0,
        tiled=True,
    ).astype(jnp.float32)
    grad_w_in, grad_w_back = (
        lax.psum_scatter(grad_w_in, "dp", scatter_dimension=0, tiled=True),
        lax.psum_scatter(grad_w_back, "dp", scatter_dimension=1, tiled=True),
    )
    grad_gain_attn = jnp.sum(grad_one_out * normed_one, axis=0)
    grad_shift_attn = jnp.sum(grad_one_out, axis=0)
    grad_one = norm_back(grad_one_out, normed_one, inv_one, gain_attn)
    grad_b_out = jnp.sum(grad_one, axis=0)
    grad_one_full = lax.all_gather(grad_one.astype(jnp.bfloat16), "tensor", axis=0, tiled=True)
    grad_w_out = matmul_over_rows(context, grad_one_full)
    grad_context = matmul_over_cols(grad_one_full, mat_out).astype(jnp.bfloat16)
    grad_query, grad_keys, grad_values = attend_backward(
        query_rows, key_rows, value_rows, context, grad_context, log_total, seg_ids, HD, block_rows
    )
    grad_b_query_part = jnp.sum(grad_query, axis=0)
    grad_b_value_part = jnp.sum(grad_values, axis=0)
    grad_query_bf = grad_query.astype(jnp.bfloat16)
    grad_keys_bf = grad_keys.astype(jnp.bfloat16)
    grad_values_bf = grad_values.astype(jnp.bfloat16)
    grad_w_query = matmul_over_rows(rows_full, grad_query_bf)
    grad_w_key = matmul_over_rows(rows_full, grad_keys_bf)
    grad_w_value = matmul_over_rows(rows_full, grad_values_bf)
    query_part = matmul_over_cols(grad_query_bf, mat_query)
    key_part = matmul_over_cols(grad_keys_bf, mat_key)
    value_part = matmul_over_cols(grad_values_bf, mat_value)
    grad_in = grad_one + lax.psum_scatter(
        (query_part + key_part + value_part).astype(jnp.bfloat16),
        "tensor",
        scatter_dimension=0,
        tiled=True,
    ).astype(jnp.float32)
    grad_w_query, grad_w_key, grad_w_value, grad_w_out = (
        lax.psum_scatter(grad_w_query, "dp", scatter_dimension=0, tiled=True),
        lax.psum_scatter(grad_w_key, "dp", scatter_dimension=0, tiled=True),
        lax.psum_scatter(grad_w_value, "dp", scatter_dimension=0, tiled=True),
        lax.psum_scatter(grad_w_out, "dp", scatter_dimension=1, tiled=True),
    )

    def widen(part_vec, full_width):
        return lax.dynamic_update_slice_in_dim(
            jnp.zeros((full_width,), jnp.float32), part_vec, tensor_index * part_vec.shape[0], 0
        )

    small_sums = lax.psum(
        (
            widen(grad_b_query_part, b_query.shape[0]),
            widen(grad_b_value_part, b_value.shape[0]),
            grad_b_out,
            grad_gain_attn,
            grad_shift_attn,
            widen(grad_b_in_part, b_in.shape[0]),
            grad_b_back,
            grad_gain_ffn,
            grad_shift_ffn,
        ),
        ("dp", "tensor"),
    )
    return (
        output,
        grad_in,
        grad_w_query,
        small_sums[0],
        grad_w_key,
        grad_w_value,
        small_sums[1],
        grad_w_out,
        small_sums[2],
        small_sums[3],
        small_sums[4],
        grad_w_in,
        small_sums[5],
        grad_w_back,
        small_sums[6],
        small_sums[7],
        small_sums[8],
    )


def solution(mesh):
    placed = (
        P(("dp", "tensor"), None),
        P("dp", None),
        P("dp", "tensor"),
        P(),
        P("dp", "tensor"),
        P("dp", "tensor"),
        P(),
        P("tensor", "dp"),
        P(),
        P(),
        P(),
        P("dp", "tensor"),
        P(),
        P("tensor", "dp"),
        P(),
        P(),
        P(),
        P(("dp", "tensor"), None),
    )
    return jax.shard_map(
        on_device,
        mesh=mesh,
        in_specs=placed,
        out_specs=(
            P(("dp", "tensor"), None),
            P(("dp", "tensor"), None),
            P("dp", "tensor"),
            P(),
            P("dp", "tensor"),
            P("dp", "tensor"),
            P(),
            P("tensor", "dp"),
            P(),
            P(),
            P(),
            P("dp", "tensor"),
            P(),
            P("tensor", "dp"),
            P(),
            P(),
            P(),
        ),
        check_vma=False,
    )
```

profile of v0, /device:TPU:0, one launch (start us, length us, event | category | flops | bytes accessed | tf_op | source)
XLA Modules:
  0.0 598.6 jit_solution(13437722508312491656)
XLA Ops:
  10.3 1.3 fusion.36
  13.0 11.6 %all_gather.37 = bf16[1024,256]{1,0:T(8,128)(2,1)S(1)} all-gather(bf16[128,256]{1,0:T(8,128)(2,1)} %param.27), channel_id=1, replica_groups=mesh['dp'=8,'tensor'=4] {'dp'}, dimensions={0}, use_global_device_ids=true | all-gather | bytes 589824 | tf_op jit(solution)/shard_map/all_gather | solution.py:210
  24.6 9.5 %all_gather.38 = bf16[1024,256]{1,0:T(8,128)(2,1)S(1)} all-gather(bf16[128,256]{1,0:T(8,128)(2,1)} %param.24), channel_id=1, replica_groups=mesh['dp'=8,'tensor'=4] {'dp'}, dimensions={0}, use_global_device_ids=true | all-gather | bytes 589824 | tf_op jit(solution)/shard_map/all_gather | solution.py:208
  34.1 9.2 %all_gather.39 = bf16[1024,256]{1,0:T(8,128)(2,1)S(1)} all-gather(bf16[128,256]{1,0:T(8,128)(2,1)} %param.26), channel_id=1, replica_groups=mesh['dp'=8,'tensor'=4] {'dp'}, dimensions={0}, use_global_device_ids=true | all-gather | bytes 589824 | tf_op jit(solution)/shard_map/all_gather | solution.py:209
  43.3 10.6 %all_gather.40 = bf16[256,1024]{1,0:T(8,128)(2,1)} all-gather(bf16[256,128]{1,0:T(8,128)(2,1)S(1)} %copy-done.33), channel_id=1, replica_groups=mesh['dp'=8,'tensor'=4] {'dp'}, dimensions={1}, use_global_device_ids=true | all-gather | bytes 589824 | tf_op jit(solution)/shard_map/all_gather | solution.py:211
  53.9 1.8 fusion.13
  57.1 4.8 while.38
  61.9 2.5 convolution_convert_fusion.3
  65.1 27.1 %reduce-scatter.11.cloned.1.call-done = bf16[128,1024]{1,0:T(8,128)(2,1)} async-done(((bf16[512,1024]{1,0:T(8,128)(2,1)}), bf16[128,1024]{1,0:T(8,128)(2,1)}) %reduce-scatter.11.cloned.1.call-update) | async-done | bytes 262160 | tf_op jit(solution)/shard_map/reduce_scatter | solution.py:221
  92.2 1.1 fusion.22
  93.3 1.2 multiply_reduce_fusion.5
  94.5 1.8 fusion.21
  97.6 27.1 %all-gather.9.cloned.1.call-done = bf16[512,1024]{1,0:T(8,128)(2,1)} async-done(((bf16[128,1024]{1,0:T(8,128)(2,1)}), bf16[512,1024]{1,0:T(8,128)(2,1)}) %all-gather.9.cloned.1.call-update) | async-done | bytes 1048592 | tf_op jit(solution)/shard_map/all_gather | solution.py:230
  124.7 4.6 multiply_convert_fusion.1
  129.3 24.4 %all-gather.13.cloned.1.call-done = bf16[1024,1024]{1,0:T(8,128)(2,1)} async-done(((bf16[1024,128]{1,0:T(8,128)(2,1)}), bf16[1024,1024]{1,0:T(8,128)(2,1)}) %all-gather.13.cloned.1.call-update) | async-done | bytes 2097168 | tf_op jit(solution)/shard_map/all_gather | solution.py:233
  153.8 3.9 convolution_convert_fusion.2
  157.7 27.4 %reduce-scatter.13.cloned.1.call-done = bf16[128,1024]{1,0:T(8,128)(2,1)} async-done(((bf16[512,1024]{1,0:T(8,128)(2,1)}), bf16[128,1024]{1,0:T(8,128)(2,1)}) %reduce-scatter.13.cloned.1.call-update) | async-done | bytes 262160 | tf_op jit(solution)/shard_map/reduce_scatter | solution.py:239
  185.1 1.3 fusion.34
  187.0 1.1 fusion.33
  188.3 26.4 %all-gather.15.cloned.1.call-done = bf16[512,1024]{1,0:T(8,128)(2,1)} async-done(((bf16[128,1024]{1,0:T(8,128)(2,1)}), bf16[512,1024]{1,0:T(8,128)(2,1)}) %all-gather.15.cloned.1.call-update) | async-done | bytes 1048592 | tf_op jit(solution)/shard_map/all_gather | solution.py:261
  214.7 5.2 fusion.37
  220.9 2.3 convolution_convert_fusion.1
  223.3 26.8 %reduce-scatter.15.cloned.1.call-done = bf16[128,1024]{1,0:T(8,128)(2,1)} async-done(((bf16[512,1024]{1,0:T(8,128)(2,1)}), bf16[128,1024]{1,0:T(8,128)(2,1)}) %reduce-scatter.15.cloned.1.call-update) | async-done | bytes 262160 | tf_op jit(solution)/shard_map/reduce_scatter | solution.py:267
  250.0 2.0 multiply_reduce_fusion.1
  252.0 1.8 fusion.32
  254.7 26.5 %all-gather.17.cloned.1.call-done = bf16[512,1024]{1,0:T(8,128)(2,1)} async-done(((bf16[128,1024]{1,0:T(8,128)(2,1)}), bf16[512,1024]{1,0:T(8,128)(2,1)}) %all-gather.17.cloned.1.call-update) | async-done | bytes 1048592 | tf_op jit(solution)/shard_map/all_gather | solution.py:281
  281.2 2.4 convolution_convert_fusion.4
  284.6 13.1 %while.39 = (s32[]{:T(128)}, f32[512,256]{0,1:T(8,128)}, f32[512,256]{0,1:T(8,128)S(1)}, f32[512,256]{0,1:T(8,128)S(1)}, bf16[512,256]{0,1:T(8,128)(2,1)S(1)}, /...) while((s32[]{:T(128)}, f32[512,256]{0,1:T(8,128)}, ...), condition=%wide.region_17.18_spmd.clone, body=%wide.region_15.17_spmd.clone.sunk | while | flops 340395520 | bytes 25846364 | solution.py:168
  297.7 2.9 convolution_bitcast_fusion.2
  300.7 1.4 convolution_bitcast_fusion.1
  302.2 1.5 convolution_bitcast_fusion
  304.8 1.6 fusion.29
  306.4 1.5 add_convert_fusion
  307.9 1.4 fusion.40
  309.5 4.5 fusion.41
  315.5 3.3 fusion.15
  319.6 1.2 reduce_sum.193
  321.4 41.4 %all-reduce = (f32[1024]{0:T(1024)}, f32[1024]{0:T(1024)}, f32[1024]{0:T(1024)}, f32[1024]{0:T(1024)}, f32[1024]{0:T(1024)}, /*index=5*/f32[4096]{0:T(1024)}, f32[1024]{0:T(1024)}, f32[1024]{0:T(1024)}, f32[1024]{0:T(1024)}) all-reduce(f32[1024]{0:T(1024)S(1)} %dynamic_update_slice.62, ...), channel_id=1, replica_groups=mesh['dp'=8,'tensor'=4] {'dp','tensor'}, use_global_device_ids=true, to_apply=%region_21.22 | all-reduce | flops 12288 | bytes 98304 | tf_op jit(solution)/shard_map/psum | solution.py:316
  362.8 1.7 copy.43
  364.4 10.7 %reduce-scatter.21.cloned.1.call-done = f32[128,256]{0,1:T(8,128)} async-done(((f32[1024,256]{0,1:T(8,128)}), f32[128,256]{0,1:T(8,128)}) %reduce-scatter.21.cloned.1.call-update) | async-done | bytes 131088 | tf_op jit(solution)/shard_map/reduce_scatter | solution.py:306
  375.2 1.7 copy.44
  376.8 37.3 %reduce-scatter.23.cloned.1.call-done = f32[128,256]{0,1:T(8,128)} async-done(((f32[1024,256]{0,1:T(8,128)}), f32[128,256]{0,1:T(8,128)}) %reduce-scatter.23.cloned.1.call-update) | async-done | bytes 131088 | tf_op jit(solution)/shard_map/reduce_scatter | solution.py:307
  414.1 1.7 copy.45
  415.8 27.8 %reduce-scatter.17.cloned.1.call-done = bf16[128,1024]{1,0:T(8,128)(2,1)} async-done(((bf16[512,1024]{1,0:T(8,128)(2,1)}), bf16[128,1024]{1,0:T(8,128)(2,1)}) %reduce-scatter.17.cloned.1.call-update) | async-done | bytes 262160 | tf_op jit(solution)/shard_map/reduce_scatter | solution.py:298
  443.6 1.8 convert_add_fusion.2
  445.4 36.2 %reduce-scatter.25.cloned.1.call-done = f32[256,128]{1,0:T(8,128)} async-done(((f32[256,1024]{1,0:T(8,128)}), f32[256,128]{1,0:T(8,128)}) %reduce-scatter.25.cloned.1.call-update) | async-done | bytes 131088 | tf_op jit(solution)/shard_map/reduce_scatter | solution.py:308
  481.6 54.9 %reduce-scatter.29.cloned.1.call-done = f32[1024,128]{1,0:T(8,128)} async-done(((f32[1024,1024]{1,0:T(8,128)}), f32[1024,128]{1,0:T(8,128)}) %reduce-scatter.29.cloned.1.call-update) | async-done | bytes 524304 | tf_op jit(solution)/shard_map/reduce_scatter | solution.py:275
  536.5 54.8 %reduce-scatter.27.cloned.1.call-done = f32[128,1024]{1,0:T(8,128)} async-done(((f32[1024,1024]{1,0:T(8,128)}), f32[128,1024]{1,0:T(8,128)}) %reduce-scatter.27.cloned.1.call-update) | async-done | bytes 524304 | tf_op jit(solution)/shard_map/reduce_scatter | solution.py:274
  (227 shorter events, 30.8 us)
Async XLA Ops:
  8.0 35.3 %copy-start.33 = (bf16[256,128]{1,0:T(8,128)(2,1)S(1)}, bf16[256,128]{1,0:T(8,128)(2,1)}, u32[]{:S(2)}) copy-start(bf16[256,128]{1,0:T(8,128)(2,1)} %param.29) | copy-start | bytes 196612
  8.0 45.8 %all-gather.7.cloned.1.call-start = ((), (), s32[]{:S(2)}) async-start(), calls=%async_computation.10 | async-start | bytes 1310720 | tf_op jit(solution)/shard_map/all_gather | solution.py:206
  8.8 83.4 %reduce-scatter.11.cloned.1.call-start = ((), (), s32[]{:S(2)}) async-start(), calls=%async_computation.11 | async-start | bytes 1310720 | tf_op jit(solution)/shard_map/reduce_scatter | solution.py:221
  24.6 31.2 %copy-start.16 = (bf16[1024,256]{1,0:T(8,128)(2,1)}, bf16[1024,256]{1,0:T(8,128)(2,1)S(1)}, u32[]{:S(2)}) copy-start(bf16[1024,256]{1,0:T(8,128)(2,1)S(1)} %all_gather.37) | copy-start | bytes 1572868
  34.1 22.2 %copy-start.19 = (bf16[1024,256]{1,0:T(8,128)(2,1)}, bf16[1024,256]{1,0:T(8,128)(2,1)S(1)}, u32[]{:S(2)}) copy-start(bf16[1024,256]{1,0:T(8,128)(2,1)S(1)} %all_gather.38) | copy-start | bytes 1572868
  43.3 13.1 %copy-start.21 = (bf16[1024,256]{1,0:T(8,128)(2,1)}, bf16[1024,256]{1,0:T(8,128)(2,1)S(1)}, u32[]{:S(2)}) copy-start(bf16[1024,256]{1,0:T(8,128)(2,1)S(1)} %all_gather.39) | copy-start | bytes 1572868
  53.9 1.9 copy-start.9
  61.8 30.3 %copy-start.2 = (bf16[128,1024]{1,0:T(8,128)(2,1)S(1)}, bf16[128,1024]{1,0:T(8,128)(2,1)}, u32[]{:S(2)}) copy-start(bf16[128,1024]{1,0:T(8,128)(2,1)} %param.22) | copy-start | bytes 786436
  61.9 30.3 %copy-start.31 = (f32[1024]{0:T(1024)S(1)}, f32[1024]{0:T(1024)}, u32[]{:S(2)}) copy-start(f32[1024]{0:T(1024)} %param.30) | copy-start | bytes 12292
  61.9 32.6 %copy-start.32 = (f32[1024]{0:T(1024)S(1)}, f32[1024]{0:T(1024)}, u32[]{:S(2)}) copy-start(f32[1024]{0:T(1024)} %param.31) | copy-start | bytes 12292
  61.9 32.6 %copy-start.34 = (f32[1024]{0:T(1024)S(1)}, f32[1024]{0:T(1024)}, u32[]{:S(2)}) copy-start(f32[1024]{0:T(1024)} %param.32) | copy-start | bytes 12292
  64.4 33.2 %all-gather.11.cloned.1.call-start = ((), (), s32[]{:S(2)}) async-start(), calls=%async_computation.13 | async-start | bytes 2359296 | tf_op jit(solution)/shard_map/all_gather | solution.py:232
  65.0 59.7 %all-gather.9.cloned.1.call-start = ((), (), s32[]{:S(2)}) async-start(), calls=%async_computation.12 | async-start | bytes 1310720 | tf_op jit(solution)/shard_map/all_gather | solution.py:230
  96.3 57.5 %all-gather.13.cloned.1.call-start = ((), (), s32[]{:S(2)}) async-start(), calls=%async_computation.14 | async-start | bytes 2359296 | tf_op jit(solution)/shard_map/all_gather | solution.py:233
  96.9 88.2 %reduce-scatter.13.cloned.1.call-start = ((), (), s32[]{:S(2)}) async-start(), calls=%async_computation.15 | async-start | bytes 1310720 | tf_op jit(solution)/shard_map/reduce_scatter | solution.py:239
  129.3 28.3 %copy-start.25 = (bf16[512,1024]{1,0:T(8,128)(2,1)}, bf16[512,1024]{1,0:T(8,128)(2,1)S(1)}, u32[]{:S(2)}) copy-start(bf16[512,1024]{1,0:T(8,128)(2,1)S(1)} %get-tuple-element.629) | copy-start | bytes 3145732
  153.8 31.3 %copy-start.11 = (bf16[128,1024]{1,0:T(8,128)(2,1)S(1)}, bf16[128,1024]{1,0:T(8,128)(2,1)}, u32[]{:S(2)}) copy-start(bf16[128,1024]{1,0:T(8,128)(2,1)} %reduce-scatter.11.cloned.1.call-done) | copy-start | bytes 786436
  153.8 31.3 %copy-start.40 = (f32[1024]{0:T(1024)S(1)}, f32[1024]{0:T(1024)}, u32[]{:S(2)}) copy-start(f32[1024]{0:T(1024)} %param.36) | copy-start | bytes 12292
  157.6 29.0 %copy-start.28 = (bf16[128,1024]{1,0:T(8,128)(2,1)S(1)}, bf16[128,1024]{1,0:T(8,128)(2,1)}, u32[]{:S(2)}) copy-start(bf16[128,1024]{1,0:T(8,128)(2,1)} %param.39) | copy-start | bytes 786436
  157.6 29.0 %copy-start.35 = (f32[1024]{0:T(1024)S(1)}, f32[1024]{0:T(1024)}, u32[]{:S(2)}) copy-start(f32[1024]{0:T(1024)} %param.37) | copy-start | bytes 12292
  157.6 29.4 %copy-start.41 = (f32[1024]{0:T(1024)S(1)}, f32[1024]{0:T(1024)}, u32[]{:S(2)}) copy-start(f32[1024]{0:T(1024)} %param.38) | copy-start | bytes 12292
  157.7 57.1 %all-gather.15.cloned.1.call-start = ((), (), s32[]{:S(2)}) async-start(), calls=%async_computation.16 | async-start | bytes 1310720 | tf_op jit(solution)/shard_map/all_gather | solution.py:261
  188.1 61.9 %reduce-scatter.15.cloned.1.call-start = ((), (), s32[]{:S(2)}) async-start(), calls=%async_computation.17 | async-start | bytes 1310720 | tf_op jit(solution)/shard_map/reduce_scatter | solution.py:267
  214.7 6.1 %copy-start.43 = (bf16[1024,1024]{1,0:T(8,128)(2,1)S(1)}, bf16[1024,1024]{1,0:T(8,128)(2,1)}, u32[]{:S(2)}) copy-start(bf16[1024,1024]{1,0:T(8,128)(2,1)} %all-gather.11.cloned.1.call-done) | copy-start | bytes 6291460
  223.2 58.0 %all-gather.17.cloned.1.call-start = ((), (), s32[]{:S(2)}) async-start(), calls=%async_computation.18 | async-start | bytes 1310720 | tf_op jit(solution)/shard_map/all_gather | solution.py:281
  250.0 31.2 %copy-start.18 = (bf16[256,1024]{1,0:T(8,128)(2,1)S(1)}, bf16[256,1024]{1,0:T(8,128)(2,1)}, u32[]{:S(2)}) copy-start(bf16[256,1024]{1,0:T(8,128)(2,1)} %all_gather.40) | copy-start | bytes 1572868
  253.8 29.8 %copy-start.14 = (f32[128,1024]{1,0:T(8,128)}, f32[128,1024]{1,0:T(8,128)S(1)}, u32[]{:S(2)}) copy-start(f32[128,1024]{1,0:T(8,128)S(1)} %get-tuple-element.615) | copy-start | bytes 1572868
  254.7 108.1 %reduce-scatter.19.cloned.1.call-start = ((), (), s32[]{:S(2)}) async-start(), calls=%async_computation.20 | async-start | bytes 1179648 | tf_op jit(solution)/shard_map/reduce_scatter | solution.py:305
  284.7 1.9 copy-start
  284.7 1.9 copy-start.23
  286.8 2.4 copy-start.1
  291.3 1.9 copy-start
  291.3 1.9 copy-start.23
  293.3 2.4 copy-start.1
  297.7 3.0 copy-start.10
  300.6 74.5 %reduce-scatter.21.cloned.1.call-start = ((), (), s32[]{:S(2)}) async-start(), calls=%async_computation.21 | async-start | bytes 1179648 | tf_op jit(solution)/shard_map/reduce_scatter | solution.py:306
  302.2 1.6 copy-start.22
  302.2 111.9 %reduce-scatter.23.cloned.1.call-start = ((), (), s32[]{:S(2)}) async-start(), calls=%async_computation.22 | async-start | bytes 1179648 | tf_op jit(solution)/shard_map/reduce_scatter | solution.py:307
  303.7 139.8 %reduce-scatter.17.cloned.1.call-start = ((), (), s32[]{:S(2)}) async-start(), calls=%async_computation.19 | async-start | bytes 1310720 | tf_op jit(solution)/shard_map/reduce_scatter | solution.py:298
  304.8 1.6 copy-start.17
  307.9 173.7 %reduce-scatter.25.cloned.1.call-start = ((), (), s32[]{:S(2)}) async-start(), calls=%async_computation.23 | async-start | bytes 1179648 | tf_op jit(solution)/shard_map/reduce_scatter | solution.py:308
  309.4 227.1 %reduce-scatter.29.cloned.1.call-start = ((), (), s32[]{:S(2)}) async-start(), calls=%async_computation.25 | async-start | bytes 4718592 | tf_op jit(solution)/shard_map/reduce_scatter | solution.py:275
  314.0 277.3 %reduce-scatter.27.cloned.1.call-start = ((), (), s32[]{:S(2)}) async-start(), calls=%async_computation.24 | async-start | bytes 4718592 | tf_op jit(solution)/shard_map/reduce_scatter | solution.py:274
  318.8 2.6 copy-start.36
  318.8 2.6 copy-start.37
  318.8 2.6 copy-start.38
  318.8 2.6 copy-start.39
  318.8 124.8 %copy-start.15 = (f32[128,1024]{1,0:T(8,128)S(1)}, f32[128,1024]{1,0:T(8,128)}, u32[]{:S(2)}) copy-start(f32[128,1024]{1,0:T(8,128)} %copy-done.14) | copy-start | bytes 1572868
  (23 other events, 27.1 us)
Sparse Core Ops, SparseCore 0:
  10.4 30.6 all-gather.6
  64.5 27.5 reduce-scatter.10
  157.8 27.2 reduce-scatter.12
  188.2 26.4 all-gather.14
  223.3 26.6 reduce-scatter.14
Sparse Core Ops, SparseCore 1:
  66.8 27.9 all-gather.10
  96.8 27.9 all-gather.8
  126.4 27.3 all-gather.12
  254.7 26.4 all-gather.16
  300.7 35.2 reduce-scatter.18
  339.2 35.9 reduce-scatter.20
  378.2 35.9 reduce-scatter.22
  416.3 27.2 reduce-scatter.16
  447.2 34.3 reduce-scatter.24
  485.5 50.9 reduce-scatter.28
  540.3 50.9 reduce-scatter.26
where the time goes:
time: 600 us; the launch traced here: 599 us
  waiting for transfers between devices  409 us (68%)
  blocking collectives  82.3 us (14%)
  matrix products  48.7 us (8%)
  other arithmetic  21.4 us (4%)
  local copies, waits for them, and re-layouts  17.9 us (3%)
  between operations  17.3 us (3%)
    reduce_scatter x1, waiting for transfers between devices, on_device(): lax.psum_scatter(grad_w_back, 'dp', scatter_dimension=1, tiled=True)  54.9 us
    reduce_scatter x1, waiting for transfers between devices, on_device(): lax.psum_scatter(grad_w_in, 'dp', scatter_dimension=0, tiled=True)  54.8 us
    psum x1, blocking collectives, on_device(): lax.psum((widen(grad_b_query_part, b_query.shape[0]), widen(grad_b_value_...  41.4 us
    reduce_scatter x1, waiting for transfers between devices, on_device(): lax.psum_scatter(grad_w_value, 'dp', scatter_dimension=0, tiled=True)  37.3 us
    reduce_scatter x1, waiting for transfers between devices, on_device(): lax.psum_scatter(grad_w_out, 'dp', scatter_dimension=1, tiled=True)  36.2 us
    reduce_scatter x1, waiting for transfers between devices, on_device(): lax.psum_scatter((query_part + key_part + value_part).astype(jnp.bfloat16...  27.8 us
    reduce_scatter x1, waiting for transfers between devices, on_device(): lax.psum_scatter(matmul_plain(activation, mat_back).astype(jnp.bfloat16),...  27.4 us
    reduce_scatter x1, waiting for transfers between devices, on_device(): lax.psum_scatter(matmul_plain(context, mat_out).astype(jnp.bfloat16), 'te...  27.1 us
  transfers between devices with their start and end apart: 16, of which 13 were waited for; matrix products, arithmetic and copies ran while one was open for 6% of the time, Pallas kernels for 0%

commit v1 on v0

--- a/solution.py
+++ b/solution.py
@@ -1,3 +1,4 @@
+import functools
 import jax
 import jax.numpy as jnp
 from jax import lax
@@ -6,6 +7,37 @@
 HD = 64
 epsilon = 1e-06
 masked_value = -1e30
+
+
+def run_ranges_now(obj, row_axis):
+    r1 = lax.axis_size(row_axis)
+    z1 = lax.axis_index(row_axis)
+    local_out, taken_in, upper = (r1, z1, obj.shape[0])
+    kept_arr = jnp.zeros(
+        [no * local_out if u == 0 else no for u, no in enumerate(obj.shape)], obj.dtype
+    )
+    x_next = lax.dynamic_update_slice_in_dim(kept_arr, obj, taken_in * upper, axis=0)
+    d_next = e_now = obj
+    q = 1
+    while q < local_out // 2 + 1:
+        d_next = lax.ppermute(
+            d_next, row_axis, perm=[(u, (u + 1) % local_out) for u in range(local_out)]
+        )
+        x_next = lax.dynamic_update_slice_in_dim(
+            x_next, d_next, (taken_in - q) % local_out * upper, axis=0
+        )
+        if 2 * q < local_out:
+            e_now = lax.ppermute(
+                e_now, axis_name=row_axis, perm=[(u, (u - 1) % local_out) for u in range(local_out)]
+            )
+            x_next = lax.dynamic_update_slice_in_dim(
+                x_next, e_now, (taken_in + q) % local_out * upper, axis=0
+            )
+        q = q + 1
+    return x_next
+
+
+load_bars = functools.partial(run_ranges_now, row_axis="tensor")
 
 
 def matmul_plain(left_side, right_side):
@@ -227,7 +259,7 @@
     resid_one = tokens.astype(jnp.float32) + attn_sum + b_out
     hidden_one, normed_one, inv_one = layer_norm(resid_one, gain_attn, shift_attn)
     hidden_bf = hidden_one.astype(jnp.bfloat16)
-    hidden_full = lax.all_gather(hidden_bf, "tensor", axis=0, tiled=True)
+    hidden_full = load_bars(hidden_bf)
     ffn_mats = (
         lax.all_gather(w_in, "dp", axis=0, tiled=True),
         lax.all_gather(w_back, "dp", axis=1, tiled=True),

time: 600 us -> 572 us (0.953)
  waiting for transfers between devices: 409 us -> 375 us
    all_gather x1 -> x0, waiting for transfers between devices: 27.1 us -> none  [on_device(): hidden_full = lax.all_gather(hidden_bf, 'tensor', axis=0, tiled=True)]
    all_gather x1, waiting for transfers between devices: 24.4 us -> 3.77 us  [on_device(): lax.all_gather(w_back, 'dp', axis=1, tiled=True)]
    ppermute x0 -> x3, waiting for transfers between devices: none -> 15.2 us  [the longest x2 13.5 us: run_ranges_now(): lax.ppermute(d_next, row_axis, perm=[(u, (u + 1) % local_out) for u in ra...]
  transfers between devices with their start and end apart: 16 -> 18, of which waited for: 13 -> 15; matrix products, arithmetic and copies ran while one was open for 6% -> 7% of each run, Pallas kernels for 0% -> 0%
where the time goes in v1:
time: 572 us; the launch traced here: 571 us
  waiting for transfers between devices  375 us (66%)
  blocking collectives  82.4 us (14%)
  matrix products  52 us (9%)
  local copies, waits for them, and re-layouts  19 us (3%)
  other arithmetic  18.7 us (3%)
  between operations  17.6 us (3%)
    reduce_scatter x1, waiting for transfers between devices, on_device(): lax.psum_scatter(grad_w_in, 'dp', scatter_dimension=0, tiled=True)  54.8 us
    reduce_scatter x1, waiting for transfers between devices, on_device(): lax.psum_scatter(grad_w_back, 'dp', scatter_dimension=1, tiled=True)  54.7 us
    psum x1, blocking collectives, on_device(): lax.psum((widen(grad_b_query_part, b_query.shape[0]), widen(grad_b_value_...  41.5 us
    reduce_scatter x1, waiting for transfers between devices, on_device(): lax.psum_scatter(grad_w_value, 'dp', scatter_dimension=0, tiled=True)  37.5 us
    reduce_scatter x1, waiting for transfers between devices, on_device(): lax.psum_scatter(grad_w_out, 'dp', scatter_dimension=1, tiled=True)  36.2 us
    reduce_scatter x1, waiting for transfers between devices, on_device(): lax.psum_scatter((query_part + key_part + value_part).astype(jnp.bfloat16...  27.9 us
    reduce_scatter x1, waiting for transfers between devices, on_device(): lax.psum_scatter(matmul_plain(activation, mat_back).astype(jnp.bfloat16),...  27.4 us
    reduce_scatter x1, waiting for transfers between devices, on_device(): lax.psum_scatter(matmul_over_cols(grad_pre_bf, mat_in).astype(jnp.bfloat1...  26.8 us
  transfers between devices with their start and end apart: 18, of which 15 were waited for; matrix products, arithmetic and copies ran while one was open for 7% of the time, Pallas kernels for 0%

profile of v1, /device:TPU:0, one launch (start us, length us, event | category | flops | bytes accessed | tf_op | source)
XLA Modules:
  0.0 570.5 jit_solution(16705907828952187201)
XLA Ops:
  10.3 1.3 fusion.39
  13.0 11.6 %all_gather.34 = bf16[1024,256]{1,0:T(8,128)(2,1)S(1)} all-gather(bf16[128,256]{1,0:T(8,128)(2,1)} %param.27), channel_id=1, replica_groups=mesh['dp'=8,'tensor'=4] {'dp'}, dimensions={0}, use_global_device_ids=true | all-gather | bytes 589824 | tf_op jit(solution)/shard_map/all_gather | solution.py:242
  24.6 9.5 %all_gather.35 = bf16[1024,256]{1,0:T(8,128)(2,1)S(1)} all-gather(bf16[128,256]{1,0:T(8,128)(2,1)} %param.24), channel_id=1, replica_groups=mesh['dp'=8,'tensor'=4] {'dp'}, dimensions={0}, use_global_device_ids=true | all-gather | bytes 589824 | tf_op jit(solution)/shard_map/all_gather | solution.py:240
  34.1 9.2 %all_gather.36 = bf16[1024,256]{1,0:T(8,128)(2,1)S(1)} all-gather(bf16[128,256]{1,0:T(8,128)(2,1)} %param.26), channel_id=1, replica_groups=mesh['dp'=8,'tensor'=4] {'dp'}, dimensions={0}, use_global_device_ids=true | all-gather | bytes 589824 | tf_op jit(solution)/shard_map/all_gather | solution.py:241
  43.3 10.6 %all_gather.37 = bf16[256,1024]{1,0:T(8,128)(2,1)} all-gather(bf16[256,128]{1,0:T(8,128)(2,1)S(1)} %copy-done.33), channel_id=1, replica_groups=mesh['dp'=8,'tensor'=4] {'dp'}, dimensions={1}, use_global_device_ids=true | all-gather | bytes 589824 | tf_op jit(solution)/shard_map/all_gather | solution.py:243
  53.9 1.8 fusion.13
  57.0 4.8 while.38
  61.9 2.5 convolution_convert_fusion.3
  65.6 26.5 %reduce-scatter.11.cloned.1.call-done = bf16[128,1024]{1,0:T(8,128)(2,1)} async-done(((bf16[512,1024]{1,0:T(8,128)(2,1)}), bf16[128,1024]{1,0:T(8,128)(2,1)}) %reduce-scatter.11.cloned.1.call-update) | async-done | bytes 262160 | tf_op jit(solution)/shard_map/reduce_scatter | solution.py:253
  92.2 1.2 fusion.22
  93.4 1.2 multiply_reduce_fusion.5
  94.9 3.8 collective-permute-start.1
  98.7 7.2 %collective-permute-done = bf16[128,1024]{1,0:T(8,128)(2,1)S(1)} collective-permute-done((bf16[128,1024]{1,0:T(8,128)(2,1)S(1)}, bf16[128,1024]{1,0:T(8,128)(2,1)S(1)}, u32[]{:S(2)}, u32[]{:S(2)}) %collective-permute-start) | collective-permute-done | bytes 262176 | tf_op jit(solution)/shard_map/ppermute | solution.py:23
  106.6 1.7 collective-permute-done.1
  109.3 6.3 %collective-permute-done.2 = bf16[128,1024]{1,0:T(8,128)(2,1)S(1)} collective-permute-done((bf16[128,1024]{1,0:T(8,128)(2,1)S(1)}, bf16[128,1024]{1,0:T(8,128)(2,1)S(1)}, u32[]{:S(2)}, u32[]{:S(2)}) %collective-permute-start.2) | collective-permute-done | bytes 262176 | tf_op jit(solution)/shard_map/ppermute | solution.py:23
  115.7 5.0 multiply_convert_fusion.1
  120.7 3.8 all-gather.10.cloned.1.call-done
  124.5 4.2 convolution_convert_fusion.2
  128.8 27.4 %reduce-scatter.13.cloned.1.call-done = bf16[128,1024]{1,0:T(8,128)(2,1)} async-done(((bf16[512,1024]{1,0:T(8,128)(2,1)}), bf16[128,1024]{1,0:T(8,128)(2,1)}) %reduce-scatter.13.cloned.1.call-update) | async-done | bytes 262160 | tf_op jit(solution)/shard_map/reduce_scatter | solution.py:271
  156.1 1.3 fusion.36
  159.4 26.4 %all-gather.12.cloned.1.call-done = bf16[512,1024]{1,0:T(8,128)(2,1)} async-done(((bf16[128,1024]{1,0:T(8,128)(2,1)}), bf16[512,1024]{1,0:T(8,128)(2,1)}) %all-gather.12.cloned.1.call-update) | async-done | bytes 1048592 | tf_op jit(solution)/shard_map/all_gather | solution.py:293
  185.8 5.2 fusion.32
  191.9 2.3 convolution_convert_fusion.1
  194.3 26.8 %reduce-scatter.15.cloned.1.call-done = bf16[128,1024]{1,0:T(8,128)(2,1)} async-done(((bf16[512,1024]{1,0:T(8,128)(2,1)}), bf16[128,1024]{1,0:T(8,128)(2,1)}) %reduce-scatter.15.cloned.1.call-update) | async-done | bytes 262160 | tf_op jit(solution)/shard_map/reduce_scatter | solution.py:299
  221.1 2.0 multiply_reduce_fusion.1
  223.1 1.8 fusion.34
  225.7 26.6 %all-gather.14.cloned.1.call-done = bf16[512,1024]{1,0:T(8,128)(2,1)} async-done(((bf16[128,1024]{1,0:T(8,128)(2,1)}), bf16[512,1024]{1,0:T(8,128)(2,1)}) %all-gather.14.cloned.1.call-update) | async-done | bytes 1048592 | tf_op jit(solution)/shard_map/all_gather | solution.py:313
  252.3 2.4 convolution_convert_fusion.4
  255.7 13.3 %while.39 = (s32[]{:T(128)}, f32[512,256]{0,1:T(8,128)}, f32[512,256]{0,1:T(8,128)S(1)}, f32[512,256]{0,1:T(8,128)S(1)}, bf16[512,256]{0,1:T(8,128)(2,1)S(1)}, /...) while((s32[]{:T(128)}, f32[512,256]{0,1:T(8,128)}, ...), condition=%wide.region_17.18_spmd.clone, body=%wide.region_15.17_spmd.clone.sunk | while | flops 340395520 | bytes 30040732 | solution.py:200
  269.1 2.9 convolution_bitcast_fusion.2
  272.0 1.5 convolution_bitcast_fusion.1
  273.6 1.5 convolution_bitcast_fusion
  275.1 1.6 fusion.29
  277.8 1.5 add_convert_fusion
  279.3 2.8 fusion.42
  282.1 4.5 fusion.15
  287.9 4.5 fusion.43
  294.0 41.5 %all-reduce = (f32[1024]{0:T(1024)}, f32[1024]{0:T(1024)}, f32[1024]{0:T(1024)}, f32[1024]{0:T(1024)}, f32[1024]{0:T(1024)}, /*index=5*/f32[4096]{0:T(1024)}, f32[1024]{0:T(1024)}, f32[1024]{0:T(1024)}, f32[1024]{0:T(1024)}) all-reduce(f32[1024]{0:T(1024)S(1)} %dynamic_update_slice.78, ...), channel_id=1, replica_groups=mesh['dp'=8,'tensor'=4] {'dp','tensor'}, use_global_device_ids=true, to_apply=%region_21.22 | all-reduce | flops 12288 | bytes 98304 | tf_op jit(solution)/shard_map/psum | solution.py:348
  335.4 1.7 copy.43
  337.1 9.5 %reduce-scatter.21.cloned.1.call-done = f32[128,256]{0,1:T(8,128)} async-done(((f32[1024,256]{0,1:T(8,128)}), f32[128,256]{0,1:T(8,128)}) %reduce-scatter.21.cloned.1.call-update) | async-done | bytes 131088 | tf_op jit(solution)/shard_map/reduce_scatter | solution.py:338
  346.6 1.7 copy.44
  348.3 37.5 %reduce-scatter.23.cloned.1.call-done = f32[128,256]{0,1:T(8,128)} async-done(((f32[1024,256]{0,1:T(8,128)}), f32[128,256]{0,1:T(8,128)}) %reduce-scatter.23.cloned.1.call-update) | async-done | bytes 131088 | tf_op jit(solution)/shard_map/reduce_scatter | solution.py:339
  385.7 1.7 copy.45
  387.4 27.9 %reduce-scatter.17.cloned.1.call-done = bf16[128,1024]{1,0:T(8,128)(2,1)} async-done(((bf16[512,1024]{1,0:T(8,128)(2,1)}), bf16[128,1024]{1,0:T(8,128)(2,1)}) %reduce-scatter.17.cloned.1.call-update) | async-done | bytes 262160 | tf_op jit(solution)/shard_map/reduce_scatter | solution.py:330
  415.3 1.8 convert_add_fusion.2
  417.1 36.2 %reduce-scatter.25.cloned.1.call-done = f32[256,128]{1,0:T(8,128)} async-done(((f32[256,1024]{1,0:T(8,128)}), f32[256,128]{1,0:T(8,128)}) %reduce-scatter.25.cloned.1.call-update) | async-done | bytes 131088 | tf_op jit(solution)/shard_map/reduce_scatter | solution.py:340
  453.4 54.8 %reduce-scatter.27.cloned.1.call-done = f32[128,1024]{1,0:T(8,128)} async-done(((f32[1024,1024]{1,0:T(8,128)}), f32[128,1024]{1,0:T(8,128)}) %reduce-scatter.27.cloned.1.call-update) | async-done | bytes 524304 | tf_op jit(solution)/shard_map/reduce_scatter | solution.py:306
  508.2 54.7 %reduce-scatter.29.cloned.1.call-done = f32[1024,128]{1,0:T(8,128)} async-done(((f32[1024,1024]{1,0:T(8,128)}), f32[1024,128]{1,0:T(8,128)}) %reduce-scatter.29.cloned.1.call-update) | async-done | bytes 524304 | tf_op jit(solution)/shard_map/reduce_scatter | solution.py:307
  (238 shorter events, 33.3 us)
Async XLA Ops:
  8.0 35.3 %copy-start.33 = (bf16[256,128]{1,0:T(8,128)(2,1)S(1)}, bf16[256,128]{1,0:T(8,128)(2,1)}, u32[]{:S(2)}) copy-start(bf16[256,128]{1,0:T(8,128)(2,1)} %param.29) | copy-start | bytes 196612
  8.0 45.8 %all-gather.6.cloned.1.call-start = ((), (), s32[]{:S(2)}) async-start(), calls=%async_computation.10 | async-start | bytes 1310720 | tf_op jit(solution)/shard_map/all_gather | solution.py:238
  8.8 83.4 %reduce-scatter.11.cloned.1.call-start = ((), (), s32[]{:S(2)}) async-start(), calls=%async_computation.11 | async-start | bytes 1310720 | tf_op jit(solution)/shard_map/reduce_scatter | solution.py:253
  24.6 31.2 %copy-start.21 = (bf16[1024,256]{1,0:T(8,128)(2,1)}, bf16[1024,256]{1,0:T(8,128)(2,1)S(1)}, u32[]{:S(2)}) copy-start(bf16[1024,256]{1,0:T(8,128)(2,1)S(1)} %all_gather.34) | copy-start | bytes 1572868
  34.1 21.7 %copy-start.26 = (bf16[1024,256]{1,0:T(8,128)(2,1)}, bf16[1024,256]{1,0:T(8,128)(2,1)S(1)}, u32[]{:S(2)}) copy-start(bf16[1024,256]{1,0:T(8,128)(2,1)S(1)} %all_gather.35) | copy-start | bytes 1572868
  43.3 13.1 %copy-start.24 = (bf16[1024,256]{1,0:T(8,128)(2,1)}, bf16[1024,256]{1,0:T(8,128)(2,1)S(1)}, u32[]{:S(2)}) copy-start(bf16[1024,256]{1,0:T(8,128)(2,1)S(1)} %all_gather.36) | copy-start | bytes 1572868
  53.9 1.9 copy-start.9
  61.8 30.3 %copy-start.2 = (bf16[128,1024]{1,0:T(8,128)(2,1)S(1)}, bf16[128,1024]{1,0:T(8,128)(2,1)}, u32[]{:S(2)}) copy-start(bf16[128,1024]{1,0:T(8,128)(2,1)} %param.22) | copy-start | bytes 786436
  61.9 30.3 %copy-start.31 = (f32[1024]{0:T(1024)S(1)}, f32[1024]{0:T(1024)}, u32[]{:S(2)}) copy-start(f32[1024]{0:T(1024)} %param.30) | copy-start | bytes 12292
  64.4 30.3 %copy-start.32 = (f32[1024]{0:T(1024)S(1)}, f32[1024]{0:T(1024)}, u32[]{:S(2)}) copy-start(f32[1024]{0:T(1024)} %param.31) | copy-start | bytes 12292
  64.4 30.3 %copy-start.34 = (f32[1024]{0:T(1024)S(1)}, f32[1024]{0:T(1024)}, u32[]{:S(2)}) copy-start(f32[1024]{0:T(1024)} %param.32) | copy-start | bytes 12292
  64.4 51.3 %all-gather.8.cloned.1.call-start = ((), (), s32[]{:S(2)}) async-start(), calls=%async_computation.12 | async-start | bytes 2359296 | tf_op jit(solution)/shard_map/all_gather | solution.py:264
  65.0 59.5 %all-gather.10.cloned.1.call-start = ((), (), s32[]{:S(2)}) async-start(), calls=%async_computation.13 | async-start | bytes 2359296 | tf_op jit(solution)/shard_map/all_gather | solution.py:265
  65.6 90.5 %reduce-scatter.13.cloned.1.call-start = ((), (), s32[]{:S(2)}) async-start(), calls=%async_computation.14 | async-start | bytes 1310720 | tf_op jit(solution)/shard_map/reduce_scatter | solution.py:271
  92.2 2.5 copy-start.11
  94.9 11.0 %collective-permute-start = (bf16[128,1024]{1,0:T(8,128)(2,1)S(1)}, bf16[128,1024]{1,0:T(8,128)(2,1)S(1)}, u32[]{:S(2)}, u32[]{:S(2)}) collective-permute-start(bf16[128,1024]{1,0:T(8,128)(2,1)S(1)} %get-tuple-element.623), channel_id=1, source_target_pairs={{0,1},{1,2},{2,3},{3,0},{4,5},{5,6},{6,7},{7,4},{8,9},{9,10},{10,1... | collective-permute-start | bytes 786440 | tf_op jit(solution)/shard_map/ppermute | solution.py:23
  94.9 13.4 %collective-permute-start.1 = (bf16[128,1024]{1,0:T(8,128)(2,1)S(1)}, bf16[128,1024]{1,0:T(8,128)(2,1)}, u32[]{:S(2)}, u32[]{:S(2)}) collective-permute-start(bf16[128,1024]{1,0:T(8,128)(2,1)S(1)} %get-tuple-element.623), channel_id=1, source_target_pairs={{0,3},{1,0},{2,1},{3,2},{4,7},{5,4},{6,5},{7,6},{8,11},{9,8},{10,9... | collective-permute-start | bytes 786440 | tf_op jit(solution)/shard_map/ppermute | solution.py:30
  105.9 9.8 %collective-permute-start.2 = (bf16[128,1024]{1,0:T(8,128)(2,1)S(1)}, bf16[128,1024]{1,0:T(8,128)(2,1)S(1)}, u32[]{:S(2)}, u32[]{:S(2)}) collective-permute-start(bf16[128,1024]{1,0:T(8,128)(2,1)S(1)} %collective-permute-done), channel_id=1, source_target_pairs={{0,1},{1,2},{2,3},{3,0},{4,5},{5,6},{6,7},{7,4},{8,9},{9,10},{10,1... | collective-permute-start | bytes 786440 | tf_op jit(solution)/shard_map/ppermute | solution.py:23
  115.7 5.1 copy-start.17
  124.5 31.6 %copy-start.40 = (f32[1024]{0:T(1024)S(1)}, f32[1024]{0:T(1024)}, u32[]{:S(2)}) copy-start(f32[1024]{0:T(1024)} %param.36) | copy-start | bytes 12292
  128.7 29.0 %copy-start.29 = (bf16[128,1024]{1,0:T(8,128)(2,1)S(1)}, bf16[128,1024]{1,0:T(8,128)(2,1)}, u32[]{:S(2)}) copy-start(bf16[128,1024]{1,0:T(8,128)(2,1)} %param.39) | copy-start | bytes 786436
  128.7 29.0 %copy-start.35 = (f32[1024]{0:T(1024)S(1)}, f32[1024]{0:T(1024)}, u32[]{:S(2)}) copy-start(f32[1024]{0:T(1024)} %param.37) | copy-start | bytes 12292
  128.7 29.3 %copy-start.41 = (f32[1024]{0:T(1024)S(1)}, f32[1024]{0:T(1024)}, u32[]{:S(2)}) copy-start(f32[1024]{0:T(1024)} %param.38) | copy-start | bytes 12292
  128.7 57.1 %all-gather.12.cloned.1.call-start = ((), (), s32[]{:S(2)}) async-start(), calls=%async_computation.15 | async-start | bytes 1310720 | tf_op jit(solution)/shard_map/all_gather | solution.py:293
  159.1 62.0 %reduce-scatter.15.cloned.1.call-start = ((), (), s32[]{:S(2)}) async-start(), calls=%async_computation.16 | async-start | bytes 1310720 | tf_op jit(solution)/shard_map/reduce_scatter | solution.py:299
  185.8 6.2 %copy-start.43 = (bf16[1024,1024]{1,0:T(8,128)(2,1)S(1)}, bf16[1024,1024]{1,0:T(8,128)(2,1)}, u32[]{:S(2)}) copy-start(bf16[1024,1024]{1,0:T(8,128)(2,1)} %all-gather.8.cloned.1.call-done) | copy-start | bytes 6291460
  194.3 58.1 %all-gather.14.cloned.1.call-start = ((), (), s32[]{:S(2)}) async-start(), calls=%async_computation.17 | async-start | bytes 1310720 | tf_op jit(solution)/shard_map/all_gather | solution.py:313
  221.1 31.2 %copy-start.23 = (bf16[256,1024]{1,0:T(8,128)(2,1)S(1)}, bf16[256,1024]{1,0:T(8,128)(2,1)}, u32[]{:S(2)}) copy-start(bf16[256,1024]{1,0:T(8,128)(2,1)} %all_gather.37) | copy-start | bytes 1572868
  224.9 29.9 %copy-start.19 = (f32[128,1024]{1,0:T(8,128)}, f32[128,1024]{1,0:T(8,128)S(1)}, u32[]{:S(2)}) copy-start(f32[128,1024]{1,0:T(8,128)S(1)} %get-tuple-element.617) | copy-start | bytes 1572868
  225.7 109.7 %reduce-scatter.19.cloned.1.call-start = ((), (), s32[]{:S(2)}) async-start(), calls=%async_computation.19 | async-start | bytes 1179648 | tf_op jit(solution)/shard_map/reduce_scatter | solution.py:337
  255.8 1.9 copy-start
  255.9 1.9 copy-start.27
  257.9 2.4 copy-start.1
  262.4 1.9 copy-start
  262.5 1.9 copy-start.27
  264.5 2.4 copy-start.1
  269.0 3.0 copy-start.10
  272.0 74.7 %reduce-scatter.21.cloned.1.call-start = ((), (), s32[]{:S(2)}) async-start(), calls=%async_computation.20 | async-start | bytes 1179648 | tf_op jit(solution)/shard_map/reduce_scatter | solution.py:338
  273.5 1.6 copy-start.14
  273.5 112.2 %reduce-scatter.23.cloned.1.call-start = ((), (), s32[]{:S(2)}) async-start(), calls=%async_computation.21 | async-start | bytes 1179648 | tf_op jit(solution)/shard_map/reduce_scatter | solution.py:339
  275.1 1.7 copy-start.25
  275.1 140.2 %reduce-scatter.17.cloned.1.call-start = ((), (), s32[]{:S(2)}) async-start(), calls=%async_computation.18 | async-start | bytes 1310720 | tf_op jit(solution)/shard_map/reduce_scatter | solution.py:330
  279.2 2.9 copy-start.18
  279.3 174.1 %reduce-scatter.25.cloned.1.call-start = ((), (), s32[]{:S(2)}) async-start(), calls=%async_computation.22 | async-start | bytes 1179648 | tf_op jit(solution)/shard_map/reduce_scatter | solution.py:340
  282.1 226.1 %reduce-scatter.27.cloned.1.call-start = ((), (), s32[]{:S(2)}) async-start(), calls=%async_computation.23 | async-start | bytes 4718592 | tf_op jit(solution)/shard_map/reduce_scatter | solution.py:306
  286.7 276.2 %reduce-scatter.29.cloned.1.call-start = ((), (), s32[]{:S(2)}) async-start(), calls=%async_computation.24 | async-start | bytes 4718592 | tf_op jit(solution)/shard_map/reduce_scatter | solution.py:307
  292.4 1.6 copy-start.39
  292.4 122.9 %copy-start.20 = (f32[128,1024]{1,0:T(8,128)S(1)}, f32[128,1024]{1,0:T(8,128)}, u32[]{:S(2)}) copy-start(f32[128,1024]{1,0:T(8,128)} %copy-done.19) | copy-start | bytes 1572868
  (27 other events, 28.6 us)
Sparse Core Ops, SparseCore 0:
  10.4 30.6 all-gather.5
  64.5 27.5 reduce-scatter.10
  128.8 27.2 reduce-scatter.12
  159.3 26.4 all-gather.11
  194.4 26.6 reduce-scatter.14
  225.8 26.4 all-gather.13
Sparse Core Ops, SparseCore 1:
  66.8 27.9 all-gather.7
  96.5 27.9 all-gather.9
  272.0 35.2 reduce-scatter.18
  310.5 36.0 reduce-scatter.20
  349.8 35.9 reduce-scatter.22
  388.1 27.2 reduce-scatter.16
  418.9 34.4 reduce-scatter.24
  457.2 50.9 reduce-scatter.26
  512.0 50.9 reduce-scatter.28
